TPU v7x, 256 devices: a whole 4x4x8 slice. The times are simulated.
256 devices in a mesh: row: 8 (over y, core), col: 32 (over z, x).
Axes of the slice: x: 4, y: 4, z: 8, core: 2. Of those that a mesh axis runs over, the one named last changes fastest.
Arguments:
- rhs: bfloat16 [6144, 6144], P('row', 'col'), may hold values from -6 to 6
- basis_left: bfloat16 [6144, 6144], P('col', 'row'), may hold values from -1 to 1, as said below
- basis_right: bfloat16 [6144, 6144], P('row', 'col'), may hold values from -1 to 1, as said below
- eig_left: float32 [6144], P('row'), may hold values from 0.1 to 4
- eig_right: float32 [6144], P('col'), may hold values from 0.1 to 4
Outputs:
- solution: bfloat16 [6144, 6144], P('col', 'row')
Inputs may be any that keep to these rules, and one draw needn't show every extreme that they name: `basis_left`: an orthogonal matrix drawn uniformly, rounded to bfloat16. `basis_right`: an orthogonal matrix drawn uniformly, rounded to bfloat16.
All inputs are finite; a program needn't handle non-finite values.
Results may differ from a plain program's by a relative error of at most 0.0085.
Values may be sent and summed in bfloat16 or wider, within the bound.
No kernel may reach another device: no remote copies, remote signals or barrier semaphores. Data moves between devices by JAX's collectives and lax.ppermute only.
A program may use at most 64 MiB of HBM per device.

v0:
```python
import jax
import jax.numpy as jnp
from jax import lax
from jax.sharding import PartitionSpec as P


def laid_out(parts, dim):
    parts = jnp.moveaxis(parts, 0, dim)
    lengths = parts.shape
    return parts.reshape(*lengths[:dim], lengths[dim] * lengths[dim + 1], *lengths[dim + 2 :])


def sent_to_all(shard, axis):
    copies = jnp.broadcast_to(shard, (lax.axis_size(axis), *shard.shape))
    return lax.all_to_all(copies, axis, split_axis=0, concat_axis=0, tiled=True)


def gathered_copies(shard, axis, dim):
    return laid_out(sent_to_all(shard, axis), dim)


def in_blocks(shard, dim, peers):
    lengths = shard.shape
    parts = shard.reshape(*lengths[:dim], peers, lengths[dim] // peers, *lengths[dim + 1 :])
    return jnp.moveaxis(parts, dim, 0)


def sent_and_summed(shard, axis, dim):
    peers = lax.axis_size(axis)
    parts = lax.all_to_all(in_blocks(shard, dim, peers), axis, 0, 0, tiled=True)
    return jnp.sum(parts.astype(jnp.float32), axis=0)


def body(rhs, basis_left, basis_right, eig_left, eig_right):
    c_strip = gathered_copies(rhs, "row", 0)
    chosen = c_strip
    first = lax.dot_general(
        lax.all_gather(basis_left, "col", axis=0, tiled=True),
        chosen,
        (((0,), (0,)), ((), ())),
        preferred_element_type=jnp.float32,
    )
    projected = first.astype(jnp.bfloat16)
    right_strip = lax.all_gather(basis_right, "row", axis=0, tiled=True)
    chosen = right_strip
    second = jnp.dot(
        lax.all_gather(projected, "col", axis=1, tiled=True),
        chosen,
        preferred_element_type=jnp.float32,
    )
    scaled = (second / (eig_left[:, None] + eig_right[None, :])).astype(jnp.bfloat16)
    scaled_strip = lax.all_gather(scaled, "col", axis=1, tiled=True)
    chosen = scaled_strip
    half_turned = sent_and_summed(
        lax.dot_general(
            chosen, basis_left, (((0,), (1,)), ((), ())), preferred_element_type=jnp.float32
        ).astype(jnp.bfloat16),
        "row",
        0,
    ).astype(jnp.bfloat16)
    half_strip = gathered_copies(half_turned, "row", 0)
    chosen = half_strip
    turned = jnp.dot(
        lax.all_gather(basis_right, "col", axis=1, tiled=True),
        chosen,
        preferred_element_type=jnp.float32,
    )
    return turned.T.astype(jnp.bfloat16)


def solution(mesh):
    in_specs = (P("row", "col"), P("col", "row"), P("row", "col"), P("row"), P("col"))
    out_specs = P("col", "row")
    return jax.shard_map(body, mesh=mesh, in_specs=in_specs, out_specs=out_specs, check_vma=False)
```

profile of v0, /device:TPU:1, one launch (start us, length us, event | category | flops | bytes accessed | tf_op | source)
XLA Modules:
  0.0 472.5 jit_solution(11340699577800707060)
XLA Ops:
  6.5 0.7 all-gather.6.cloned.1.call-update
  7.3 0.7 all-gather.10.cloned.1.call-update
  8.0 0.0 all-gather.8.cloned.1.call-start
  8.1 1.1 broadcast_in_dim.8
  9.2 34.7 %all_to_all.15 = bf16[8,768,192]{1,2,0:T(8,128)(2,1)S(1)} all-to-all(bf16[8,768,192]{1,2,0:T(8,128)(2,1)S(1)} %broadcast_in_dim.8), channel_id=1, replica_groups=mesh['row'=8,'col'=32] {'row'}, dimensions={0} | all-to-all | bytes 4718592 | tf_op jit(solution)/shard_map/all_to_all | solution.py:15
  43.9 0.3 copy.15
  44.2 71.9 %all-gather.6.cloned.1.call-done = bf16[6144,768]{1,0:T(8,128)(2,1)} async-done(((bf16[192,768]{1,0:T(8,128)(2,1)}), bf16[6144,768]{1,0:T(8,128)(2,1)}) %all-gather.6.cloned.1.call-update) | async-done | bytes 9437200 | tf_op jit(solution)/shard_map/all_gather | solution.py:38
  116.1 6.4 %convolution_convert_fusion.1 = bf16[768,192]{0,1:T(8,128)(2,1)} fusion(bf16[6144,192]{0,1:T(8,128)(2,1)S(1)} %bitcast.19, bf16[6144,768]{1,0:T(8,128)(2,1)} %all-gather.6.cloned.1.call-done), kind=kOutput, calls=%fused_computation.2 | convolution fusion | flops 1812086784 | bytes 12091392 | tf_op jit(solution)/shard_map/dot_general | solution.py:37
  122.5 0.0 all-gather.12.cloned.1.call-start
  122.6 21.8 %all-gather.10.cloned.1.call-done = bf16[6144,192]{0,1:T(8,128)(2,1)} async-done(((bf16[768,192]{0,1:T(8,128)(2,1)}), bf16[6144,192]{0,1:T(8,128)(2,1)}) %all-gather.10.cloned.1.call-update) | async-done | bytes 2359312 | tf_op jit(solution)/shard_map/all_gather | solution.py:44
  144.3 105.2 %all-gather.8.cloned.1.call-done = bf16[768,6144]{0,1:T(8,128)(2,1)} async-done(((bf16[768,192]{0,1:T(8,128)(2,1)}), bf16[768,6144]{0,1:T(8,128)(2,1)}) %all-gather.8.cloned.1.call-update) | async-done | bytes 9437200 | tf_op jit(solution)/shard_map/all_gather | solution.py:47
  249.5 7.1 %fusion = bf16[768,192]{0,1:T(8,128)(2,1)} fusion(bf16[6144,192]{0,1:T(8,128)(2,1)} %all-gather.10.cloned.1.call-done, bf16[768,6144]{0,1:T(8,128)(2,1)} %all-gather.8.cloned.1.call-done, f32[192]{0:T(256)S(1)} %copy-done.2, f32[768]{0:T(1024)S(1)} %copy-done.1), kind=kOutput, calls=%fused_computation.5 | convolution fusion | flops 1812381696 | bytes 12095232 | tf_op jit(solution)/shard_map/dot_general | solution.py:46
  256.6 0.0 all-gather.14.cloned.1.call-start
  256.7 0.5 all-gather.14.cloned.1.call-update
  257.2 99.8 %all-gather.12.cloned.1.call-done = bf16[768,6144]{0,1:T(8,128)(2,1)} async-done(((bf16[768,192]{0,1:T(8,128)(2,1)}), bf16[768,6144]{0,1:T(8,128)(2,1)}) %all-gather.12.cloned.1.call-update) | async-done | bytes 9437200 | tf_op jit(solution)/shard_map/all_gather | solution.py:52
  357.0 6.9 %convolution_convert_fusion = bf16[6144,192]{0,1:T(8,128)(2,1)S(1)} fusion(bf16[768,6144]{0,1:T(8,128)(2,1)} %all-gather.12.cloned.1.call-done, bf16[192,768]{1,0:T(8,128)(2,1)S(1)} %copy-done), kind=kOutput, calls=%fused_computation | convolution fusion | flops 1813118976 | bytes 12091392 | tf_op jit(solution)/shard_map/dot_general | solution.py:55
  363.9 0.2 copy.18
  364.0 34.5 %all_to_all.16 = bf16[8,768,192]{1,2,0:T(8,128)(2,1)S(1)} all-to-all(bf16[8,768,192]{1,2,0:T(8,128)(2,1)S(1)} %bitcast.17), channel_id=1, replica_groups=mesh['row'=8,'col'=32] {'row'}, dimensions={0} | all-to-all | bytes 4718592 | tf_op jit(solution)/shard_map/all_to_all | solution.py:30
  398.5 0.4 reduce_sum.12
  398.9 0.2 broadcast_in_dim.9
  399.1 32.5 %all_to_all.17 = bf16[8,768,192]{1,2,0:T(8,128)(2,1)S(1)} all-to-all(bf16[8,768,192]{1,2,0:T(8,128)(2,1)S(1)} %broadcast_in_dim.9), channel_id=1, replica_groups=mesh['row'=8,'col'=32] {'row'}, dimensions={0} | all-to-all | bytes 4718592 | tf_op jit(solution)/shard_map/all_to_all | solution.py:15
  431.6 0.3 copy.16
  431.9 27.7 %all-gather.14.cloned.1.call-done = bf16[768,6144]{0,1:T(8,128)(2,1)} async-done(((bf16[768,192]{0,1:T(8,128)(2,1)}), bf16[768,6144]{0,1:T(8,128)(2,1)}) %all-gather.14.cloned.1.call-update) | async-done | bytes 9437200 | tf_op jit(solution)/shard_map/all_gather | solution.py:64
  459.6 6.4 %convolution_convert_fusion.2 = bf16[192,768]{1,0:T(8,128)(2,1)} fusion(bf16[6144,192]{0,1:T(8,128)(2,1)S(1)} %bitcast.20, bf16[768,6144]{0,1:T(8,128)(2,1)} %all-gather.14.cloned.1.call-done), kind=kOutput, calls=%fused_computation.3 | convolution fusion | flops 1812086784 | bytes 12091392 | tf_op jit(solution)/shard_map/dot_general | solution.py:63
  (10 shorter events, 0.1 us)
Async XLA Ops:
  6.5 109.5 %all-gather.6.cloned.1.call-start = ((), (), s32[]{:S(2)}) async-start(), calls=%async_computation.3 | async-start | bytes 9732096 | tf_op jit(solution)/shard_map/all_gather | solution.py:38
  7.3 137.1 %all-gather.10.cloned.1.call-start = ((), (), s32[]{:S(2)}) async-start(), calls=%async_computation.5 | async-start | bytes 2654208 | tf_op jit(solution)/shard_map/all_gather | solution.py:44
  8.0 241.5 %all-gather.8.cloned.1.call-start = ((), (), s32[]{:S(2)}) async-start(), calls=%async_computation.4 | async-start | bytes 9732096 | tf_op jit(solution)/shard_map/all_gather | solution.py:47
  116.1 133.4 %copy-start.1 = (f32[768]{0:T(1024)S(1)}, f32[768]{0:T(1024)}, u32[]{:S(2)}) copy-start(f32[768]{0:T(1024)} %param.8) | copy-start | bytes 9220
  116.1 133.4 %copy-start.2 = (f32[192]{0:T(256)S(1)}, f32[192]{0:T(256)}, u32[]{:S(2)}) copy-start(f32[192]{0:T(256)} %param.9) | copy-start | bytes 2308
  122.5 234.5 %copy-start = (bf16[192,768]{1,0:T(8,128)(2,1)S(1)}, bf16[192,768]{1,0:T(8,128)(2,1)}, u32[]{:S(2)}) copy-start(bf16[192,768]{1,0:T(8,128)(2,1)} %param.6) | copy-start | bytes 884740
  122.5 234.5 %all-gather.12.cloned.1.call-start = ((), (), s32[]{:S(2)}) async-start(), calls=%async_computation.6 | async-start | bytes 9732096 | tf_op jit(solution)/shard_map/all_gather | solution.py:52
  256.6 203.0 %all-gather.14.cloned.1.call-start = ((), (), s32[]{:S(2)}) async-start(), calls=%async_computation.7 | async-start | bytes 9732096 | tf_op jit(solution)/shard_map/all_gather | solution.py:64
Sparse Core Ops, SparseCore 0:
  9.9 106.1 all-gather.5
  117.9 26.3 all-gather.9
  146.9 102.5 all-gather.7
  256.7 100.1 all-gather.11
  359.4 100.1 all-gather.13
where the time goes:
time: 473 us
  waiting for transfers between devices  328 us (69%)
  blocking collectives  102 us (22%)
  matrix products  26.8 us (6%)
  between operations  13.2 us (3%)
    all_gather x1, waiting for transfers between devices, body(): lax.all_gather(projected, 'col', axis=1, tiled=True)  105 us
    all_gather x1, waiting for transfers between devices, body(): scaled_strip = lax.all_gather(scaled, 'col', axis=1, tiled=True)  99.8 us
    all_gather x1, waiting for transfers between devices, body(): lax.all_gather(basis_left, 'col', axis=0, tiled=True)  71.9 us
    all_to_all x2, blocking collectives, sent_to_all(): return lax.all_to_all(copies, axis, split_axis=0, concat_axis=0, tiled=True)  67.3 us
    all_to_all x1, blocking collectives, sent_and_summed(): parts = lax.all_to_all(in_blocks(shard, dim, peers), axis, 0, 0, tiled=True)  34.5 us
    all_gather x1, waiting for transfers between devices, body(): lax.all_gather(basis_right, 'col', axis=1, tiled=True)  27.7 us
    all_gather x1, waiting for transfers between devices, body(): right_strip = lax.all_gather(basis_right, 'row', axis=0, tiled=True)  21.8 us
  transfers between devices with their start and end apart: 5, of which 5 were waited for; matrix products, arithmetic and copies ran while one was open for 3% of the time, Pallas kernels for 0%

commit v1 on v0

v1 whole, which is shorter than its diff:
```python
import jax
import jax.numpy as jnp
from jax import lax
from jax.sharding import Mesh, PartitionSpec as P

F32, BF16 = jnp.float32, jnp.bfloat16
ROW = ("y", "core")


def dot(a, b, over):
    return lax.dot_general(a, b, ((over[:1], over[1:]), ((), ())), preferred_element_type=F32)


def gathered(shard, axis, dim):
    copies = jnp.broadcast_to(shard, (lax.axis_size(axis), *shard.shape))
    parts = lax.all_to_all(copies, axis, 0, 0, tiled=True)
    if dim == 0:
        return parts.reshape(-1, parts.shape[-1])
    return jnp.moveaxis(parts, 0, 1).reshape(parts.shape[1], -1)


def summed(partial, axis):
    peers = lax.axis_size(axis)
    parts = partial.reshape(peers, partial.shape[0] // peers, partial.shape[1])
    parts = lax.all_to_all(parts, axis, 0, 0, tiled=True)
    return jnp.sum(parts.astype(F32), axis=0)


def body(rhs, basis_left, basis_right, eig_left, eig_right):
    row_of = [(z * 8 + r, r * 8 + z) for z in range(8) for r in range(8)]
    left = lax.all_gather(basis_left, "z", axis=0, tiled=True)
    c_part = lax.all_to_all(rhs, "x", 0, 1, tiled=True)
    c_block = gathered(c_part, ROW, 0)
    turned = lax.ppermute(basis_right, (*ROW, "z"), row_of)
    right = lax.all_gather(turned, ROW, axis=1, tiled=True)
    part = dot(left, c_block, (0, 0)).astype(BF16)
    projected = gathered(summed(part, "x").astype(BF16), "x", 0)
    part = dot(projected, right, (1, 0)).astype(BF16)
    second = lax.psum_scatter(part, "z", scatter_dimension=1, tiled=True).astype(F32)
    scaled = (second / (eig_left[:, None] + eig_right[None, :])).astype(BF16)
    basis_right, _ = lax.optimization_barrier((basis_right, part))
    right = lax.all_gather(basis_right, "x", axis=1, tiled=True)
    scaled = gathered(scaled, "x", 1)
    part = dot(left, scaled, (1, 0)).astype(BF16)
    half = summed(part, "core").astype(BF16)
    half = summed(half, "y").astype(BF16)
    half = gathered(gathered(half, "y", 0), "core", 0)
    part = dot(half, right, (1, 1)).astype(BF16)
    return lax.psum_scatter(part, "z", scatter_dimension=0, tiled=True)


def solution(mesh):
    split = Mesh(mesh.devices.reshape(4, 2, 8, 4), ("y", "core", "z", "x"))
    row, col = ROW, ("z", "x")
    in_specs = (P(row, col), P(col, row), P(row, col), P(row), P(col))
    return jax.shard_map(body, mesh=split, in_specs=in_specs, out_specs=P(col, row), check_vma=False)
```

time: 473 us -> 284 us (0.60)
  waiting for transfers between devices: 328 us -> 146 us
  blocking collectives: 102 us -> 59.7 us
  starting transfers between devices: 0.16 us -> 31.7 us
  matrix products: 26.8 us -> 14.1 us
  local copies, waits for them, and re-layouts: 1.97 us -> 11.8 us
    all_gather x5 -> x3, waiting for transfers between devices: 326 us -> 10.5 us  [the longest x1 7.77 us: body(): right = lax.all_gather(turned, ROW, axis=1, tiled=True)]
    all_to_all x0 -> x5, waiting for transfers between devices: none -> 53.9 us  [the longest x3 36.7 us: gathered(): parts = lax.all_to_all(copies, axis, 0, 0, tiled=True)]
    unnamed x5 -> x6, waiting for transfers between devices: 1.97 us -> 46.6 us
    all_to_all x3 -> x4, blocking collectives: 102 us -> 59.7 us  [the longest x2 30.9 us: gathered(): parts = lax.all_to_all(copies, axis, 0, 0, tiled=True)]
    reduce_scatter x0 -> x1, waiting for transfers between devices: none -> 35.1 us  [body(): return lax.psum_scatter(part, 'z', scatter_dimension=0, tiled=True)]
    all_to_all x0 -> x5, starting transfers between devices: none -> 27.2 us  [the longest x3 18 us: gathered(): parts = lax.all_to_all(copies, axis, 0, 0, tiled=True)]
    dot_general x4, matrix products: 26.8 us -> 14.1 us  [dot(): lax.dot_general(a, b, ((over[:1], over[1:]), ((), ())), preferred_element...]
    unnamed x6 -> x10, local copies, waits for them, and re-layouts: 0.01 us -> 5.05 us
  transfers between devices with their start and end apart: 5 -> 11, of which waited for: 5 -> 9; matrix products, arithmetic and copies ran while one was open for 3% -> 4% of each run, Pallas kernels for 0% -> 0%
where the time goes in v1:
time: 284 us; the launch traced here: 279 us
  waiting for transfers between devices  146 us (51%)
  blocking collectives  59.7 us (21%)
  starting transfers between devices  31.7 us (11%)
  matrix products  14.1 us (5%)
  between operations  13.2 us (5%)
  local copies, waits for them, and re-layouts  11.8 us (4%)
  other arithmetic  2.88 us (1%)
    unnamed x6, waiting for transfers between devices  46.6 us
    all_to_all x3, waiting for transfers between devices, gathered(): parts = lax.all_to_all(copies, axis, 0, 0, tiled=True)  36.7 us
    reduce_scatter x1, waiting for transfers between devices, body(): return lax.psum_scatter(part, 'z', scatter_dimension=0, tiled=True)  35.1 us
    all_to_all x2, blocking collectives, gathered(): parts = lax.all_to_all(copies, axis, 0, 0, tiled=True)  30.9 us
    all_to_all x2, blocking collectives, summed(): parts = lax.all_to_all(parts, axis, 0, 0, tiled=True)  28.8 us
    all_to_all x3, starting transfers between devices, gathered(): parts = lax.all_to_all(copies, axis, 0, 0, tiled=True)  18 us
    all_to_all x1, waiting for transfers between devices, summed(): parts = lax.all_to_all(parts, axis, 0, 0, tiled=True)  15.4 us
    dot_general x4, matrix products, dot(): lax.dot_general(a, b, ((over[:1], over[1:]), ((), ())), preferred_element...  14.1 us
  transfers between devices with their start and end apart: 11, of which 9 were waited for; matrix products, arithmetic and copies ran while one was open for 4% of the time, Pallas kernels for 0%

profile of v1, /device:TPU:1, one launch (start us, length us, event | category | flops | bytes accessed | tf_op | source)
XLA Modules:
  0.0 279.5 jit_solution(11018644528555109359)
XLA Ops:
  7.3 1.9 copy.19
  9.1 4.8 %all-to-all-start = ((bf16[4,192,192]{2,1,0:T(8,128)(2,1)}), bf16[4,192,192]{2,1,0:T(8,128)(2,1)S(1)}, u32[]{:S(2)}, u32[]{:S(2)}) async-start(bf16[4,192,192]{2,1,0:T(8,128)(2,1)} %bitcast), calls=%async_computation | async-start | bytes 786432 | tf_op jit(solution)/shard_map/all_to_all | solution.py:32
  14.0 4.4 %collective-permute-start = (bf16[768,192]{0,1:T(8,128)(2,1)}, bf16[768,192]{0,1:T(8,128)(2,1)S(1)}, u32[]{:S(2)}, u32[]{:S(2)}) collective-permute-start(bf16[768,192]{0,1:T(8,128)(2,1)} %param.7), channel_id=1, source_target_pairs={{0,0},{4,32},{8,64},{12,96},{16,128},{20,160},{24,192},{28,224},{3... | collective-permute-start | bytes 884744 | tf_op jit(solution)/shard_map/ppermute | solution.py:34
  22.5 8.1 %all-to-all-start.1 = ((bf16[8,192,768]{2,1,0:T(8,128)(2,1)}), bf16[8,192,768]{2,1,0:T(8,128)(2,1)S(1)}, u32[]{:S(2)}, u32[]{:S(2)}) async-start(bf16[8,192,768]{2,1,0:T(8,128)(2,1)} %broadcast_in_dim.17), calls=%async_computation.1 | async-start | bytes 4718592 | tf_op jit(solution)/shard_map/all_to_all | solution.py:16
  31.3 30.3 %all-to-all-done.1 = bf16[8,192,768]{2,1,0:T(8,128)(2,1)S(1)} async-done(((bf16[8,192,768]{2,1,0:T(8,128)(2,1)}), bf16[8,192,768]{2,1,0:T(8,128)(2,1)S(1)}, u32[]{:S(2)}, u32[]{:S(2)}) %all-to-all-start.1) | async-done | bytes 2359328 | tf_op jit(solution)/shard_map/all_to_all | solution.py:16
  61.5 2.7 all-gather.4.cloned.1.call-done
  64.3 3.7 %convolution_convert_fusion.3 = bf16[768,768]{1,0:T(8,128)(2,1)S(1)} fusion(bf16[1536,768]{1,0:T(8,128)(2,1)} %all-gather.4.cloned.1.call-done, bf16[1536,768]{1,0:T(8,128)(2,1)S(1)} %bitcast.30), kind=kOutput, calls=%fused_computation.4 | convolution fusion | flops 1812529152 | bytes 5898240 | tf_op jit(solution)/shard_map/dot_general | solution.py:11
  68.0 16.8 %all_to_all.59 = bf16[4,192,768]{2,1,0:T(8,128)(2,1)S(1)} all-to-all(bf16[4,192,768]{2,1,0:T(8,128)(2,1)S(1)} %bitcast.36), channel_id=1, replica_groups=mesh['y'=4,'core'=2,'z'=8,'x'=4] {'x'}, dimensions={0} | all-to-all | bytes 2359296 | tf_op jit(solution)/shard_map/all_to_all | solution.py:25
  86.2 3.5 %all-to-all-start.3 = ((bf16[4,192,768]{2,1,0:T(8,128)(2,1)}), bf16[4,192,768]{2,1,0:T(8,128)(2,1)S(1)}, u32[]{:S(2)}, u32[]{:S(2)}) async-start(bf16[4,192,768]{2,1,0:T(8,128)(2,1)} %broadcast_in_dim.18), calls=%async_computation.3 | async-start | bytes 2359296 | tf_op jit(solution)/shard_map/all_to_all | solution.py:16
  89.7 7.8 %all-gather.6.cloned.1.call-done = bf16[768,1536]{0,1:T(8,128)(2,1)} async-done(((bf16[768,192]{0,1:T(8,128)(2,1)}), bf16[768,1536]{0,1:T(8,128)(2,1)}) %all-gather.6.cloned.1.call-update) | async-done | bytes 2359312 | tf_op jit(solution)/shard_map/all_gather | solution.py:35
  97.5 3.8 %all-to-all-done.3 = bf16[4,192,768]{2,1,0:T(8,128)(2,1)S(1)} async-done(((bf16[4,192,768]{2,1,0:T(8,128)(2,1)}), bf16[4,192,768]{2,1,0:T(8,128)(2,1)S(1)}, u32[]{:S(2)}, u32[]{:S(2)}) %all-to-all-start.3) | async-done | bytes 1179680 | tf_op jit(solution)/shard_map/all_to_all | solution.py:16
  101.3 3.7 %convolution_convert_fusion.2 = bf16[768,1536]{1,0:T(8,128)(2,1)S(1)} fusion(bf16[768,768]{1,0:T(8,128)(2,1)S(1)} %bitcast.34, bf16[768,1536]{0,1:T(8,128)(2,1)} %all-gather.6.cloned.1.call-done), kind=kOutput, calls=%fused_computation.2 | convolution fusion | flops 1813118976 | bytes 5898240 | tf_op jit(solution)/shard_map/dot_general | solution.py:11
  105.0 2.5 copy.25
  107.4 45.2 %reduce-scatter.7.cloned.1.call-done = bf16[192,768]{1,0:T(8,128)(2,1)} async-done(((bf16[1536,768]{1,0:T(8,128)(2,1)}), bf16[192,768]{1,0:T(8,128)(2,1)}) %reduce-scatter.7.cloned.1.call-update) | async-done | bytes 294928
  153.9 13.7 %all_to_all.60 = bf16[4,768,192]{1,2,0:T(8,128)(2,1)S(1)} all-to-all(bf16[4,768,192]{1,2,0:T(8,128)(2,1)S(1)} %broadcast_in_dim.19), channel_id=1, replica_groups=mesh['y'=4,'core'=2,'z'=8,'x'=4] {'x'}, dimensions={0} | all-to-all | bytes 2359296 | tf_op jit(solution)/shard_map/all_to_all | solution.py:16
  167.6 2.0 convolution_convert_fusion.1
  169.8 12.0 %all_to_all.61 = bf16[2,768,768]{1,2,0:T(8,128)(2,1)S(1)} all-to-all(bf16[2,768,768]{1,2,0:T(8,128)(2,1)S(1)} %bitcast.28), channel_id=1, replica_groups=mesh['y'=4,'core'=2,'z'=8,'x'=4] {'core'}, dimensions={0} | all-to-all | bytes 4718592 | tf_op jit(solution)/shard_map/all_to_all | solution.py:25
  184.5 4.4 %all-to-all-start.6 = ((bf16[4,192,768]{2,1,0:T(8,128)(2,1)}), bf16[4,192,768]{2,1,0:T(8,128)(2,1)S(1)}, u32[]{:S(2)}, u32[]{:S(2)}) async-start(bf16[4,192,768]{2,1,0:T(8,128)(2,1)} %bitcast.8), calls=%async_computation.6 | async-start | bytes 2359296 | tf_op jit(solution)/shard_map/all_to_all | solution.py:25
  189.4 15.4 %all-to-all-done.6 = bf16[4,192,768]{2,1,0:T(8,128)(2,1)S(1)} async-done(((bf16[4,192,768]{2,1,0:T(8,128)(2,1)}), bf16[4,192,768]{2,1,0:T(8,128)(2,1)S(1)}, u32[]{:S(2)}, u32[]{:S(2)}) %all-to-all-start.6) | async-done | bytes 1179680 | tf_op jit(solution)/shard_map/all_to_all | solution.py:25
  205.2 17.2 %all_to_all.62 = bf16[4,192,768]{2,1,0:T(8,128)(2,1)S(1)} all-to-all(bf16[4,192,768]{2,1,0:T(8,128)(2,1)S(1)} %broadcast_in_dim.20), channel_id=1, replica_groups=mesh['y'=4,'core'=2,'z'=8,'x'=4] {'y'}, dimensions={0} | all-to-all | bytes 2359296 | tf_op jit(solution)/shard_map/all_to_all | solution.py:16
  224.0 6.4 %all-to-all-start.8 = ((bf16[2,768,768]{2,1,0:T(8,128)(2,1)}), bf16[2,768,768]{2,1,0:T(8,128)(2,1)S(1)}, u32[]{:S(2)}, u32[]{:S(2)}) async-start(bf16[2,768,768]{2,1,0:T(8,128)(2,1)} %broadcast_in_dim.21), calls=%async_computation.8 | async-start | bytes 4718592 | tf_op jit(solution)/shard_map/all_to_all | solution.py:16
  230.4 2.7 all-to-all-done.8
  233.1 4.7 %convolution_convert_fusion = bf16[1536,768]{1,0:T(8,128)(2,1)} fusion(bf16[1536,768]{1,0:T(8,128)(2,1)S(1)} %bitcast.31, bf16[768,768]{0,1:T(8,128)(2,1)} %all-gather.8.cloned.1.call-done), kind=kOutput, calls=%fused_computation | convolution fusion | flops 1813118976 | bytes 5898240 | tf_op jit(solution)/shard_map/dot_general | solution.py:11
  237.8 35.1 %reduce-scatter.5.cloned.1.call-done = bf16[192,768]{1,0:T(8,128)(2,1)} async-done(((bf16[1536,768]{1,0:T(8,128)(2,1)}), bf16[192,768]{1,0:T(8,128)(2,1)}) %reduce-scatter.5.cloned.1.call-update) | async-done | bytes 294928 | tf_op jit(solution)/shard_map/reduce_scatter | solution.py:49
  (34 shorter events, 13.5 us)
Async XLA Ops:
  6.5 57.7 %all-gather.4.cloned.1.call-start = ((), (), s32[]{:S(2)}) async-start(), calls=%async_computation.11 | async-start | bytes 2654208 | tf_op jit(solution)/shard_map/all_gather | solution.py:31
  9.1 11.1 %all-to-all-start = ((bf16[4,192,192]{2,1,0:T(8,128)(2,1)}), bf16[4,192,192]{2,1,0:T(8,128)(2,1)S(1)}, u32[]{:S(2)}, u32[]{:S(2)}) async-start(bf16[4,192,192]{2,1,0:T(8,128)(2,1)} %bitcast), calls=%async_computation | async-start | bytes 786432 | tf_op jit(solution)/shard_map/all_to_all | solution.py:32
  14.0 16.6 %collective-permute-start = (bf16[768,192]{0,1:T(8,128)(2,1)}, bf16[768,192]{0,1:T(8,128)(2,1)S(1)}, u32[]{:S(2)}, u32[]{:S(2)}) collective-permute-start(bf16[768,192]{0,1:T(8,128)(2,1)} %param.7), channel_id=1, source_target_pairs={{0,0},{4,32},{8,64},{12,96},{16,128},{20,160},{24,192},{28,224},{3... | collective-permute-start | bytes 884744 | tf_op jit(solution)/shard_map/ppermute | solution.py:34
  22.5 39.1 %all-to-all-start.1 = ((bf16[8,192,768]{2,1,0:T(8,128)(2,1)}), bf16[8,192,768]{2,1,0:T(8,128)(2,1)S(1)}, u32[]{:S(2)}, u32[]{:S(2)}) async-start(bf16[8,192,768]{2,1,0:T(8,128)(2,1)} %broadcast_in_dim.17), calls=%async_computation.1 | async-start | bytes 4718592 | tf_op jit(solution)/shard_map/all_to_all | solution.py:16
  30.5 67.0 %all-gather.6.cloned.1.call-start = ((), (), s32[]{:S(2)}) async-start(), calls=%async_computation.12 | async-start | bytes 2654208 | tf_op jit(solution)/shard_map/all_gather | solution.py:35
  30.5 0.7 copy-start
  86.2 15.1 %all-to-all-start.3 = ((bf16[4,192,768]{2,1,0:T(8,128)(2,1)}), bf16[4,192,768]{2,1,0:T(8,128)(2,1)S(1)}, u32[]{:S(2)}, u32[]{:S(2)}) async-start(bf16[4,192,768]{2,1,0:T(8,128)(2,1)} %broadcast_in_dim.18), calls=%async_computation.3 | async-start | bytes 2359296 | tf_op jit(solution)/shard_map/all_to_all | solution.py:16
  89.7 63.0 %reduce-scatter.7.cloned.1.call-start = ((), (), s32[]{:S(2)}) async-start(), calls=%async_computation.15 | async-start | bytes 2654208
  107.4 45.3 %copy-start.1 = (f32[768]{0:T(1024)S(1)}, f32[768]{0:T(1024)}, u32[]{:S(2)}) copy-start(f32[768]{0:T(1024)} %param.8) | copy-start | bytes 9220
  107.4 45.3 %copy-start.2 = (f32[192]{0:T(256)S(1)}, f32[192]{0:T(256)}, u32[]{:S(2)}) copy-start(f32[192]{0:T(256)} %param.9) | copy-start | bytes 2308
  107.4 60.1 %copy-start.3 = (bf16[1536,768]{1,0:T(8,128)(2,1)S(1)}, bf16[1536,768]{1,0:T(8,128)(2,1)}, u32[]{:S(2)}) copy-start(bf16[1536,768]{1,0:T(8,128)(2,1)} %all-gather.4.cloned.1.call-done) | copy-start | bytes 7077892
  184.5 20.3 %all-to-all-start.6 = ((bf16[4,192,768]{2,1,0:T(8,128)(2,1)}), bf16[4,192,768]{2,1,0:T(8,128)(2,1)S(1)}, u32[]{:S(2)}, u32[]{:S(2)}) async-start(bf16[4,192,768]{2,1,0:T(8,128)(2,1)} %bitcast.8), calls=%async_computation.6 | async-start | bytes 2359296 | tf_op jit(solution)/shard_map/all_to_all | solution.py:25
  188.9 41.6 %all-gather.8.cloned.1.call-start = ((), (), s32[]{:S(2)}) async-start(), calls=%async_computation.13 | async-start | bytes 1474560 | tf_op jit(solution)/shard_map/all_gather | solution.py:42
  224.0 9.1 %all-to-all-start.8 = ((bf16[2,768,768]{2,1,0:T(8,128)(2,1)}), bf16[2,768,768]{2,1,0:T(8,128)(2,1)S(1)}, u32[]{:S(2)}, u32[]{:S(2)}) async-start(bf16[2,768,768]{2,1,0:T(8,128)(2,1)} %broadcast_in_dim.21), calls=%async_computation.8 | async-start | bytes 4718592 | tf_op jit(solution)/shard_map/all_to_all | solution.py:16
  230.4 42.5 %reduce-scatter.5.cloned.1.call-start = ((), (), s32[]{:S(2)}) async-start(), calls=%async_computation.14 | async-start | bytes 2654208 | tf_op jit(solution)/shard_map/reduce_scatter | solution.py:49
Sparse Core Ops, SparseCore 0:
  9.1 55.0 all-gather.3
  66.1 31.3 all-gather.5
  107.6 45.0 reduce-scatter.6
  191.1 23.3 all-gather.7
  237.9 34.9 reduce-scatter.4
